TPU v7x, 256 devices: a whole 4x4x8 slice. The times are simulated.
256 devices in a mesh: gx: 16 (over z, x_lo), gy: 8 (over y, x_hi), gz: 2 (over core).
Axes of the slice: x: 4 (x_hi: 2, x_lo: 2; x = x_hi * 2 + x_lo), y: 4, z: 8, core: 2. Of those that a mesh axis runs over, the one named last changes fastest.
Arguments:
- patches: bfloat16 [16, 8, 3, 64, 64, 256], P(None, 'gy', None, 'gx', None, 'gz'), may hold values from -8 to 308
Outputs:
- smooth: float32 [3, 512, 256, 128], P(None, 'gx', 'gy', 'gz')
- confidence: float32 [512, 256, 128], P('gx', 'gy', 'gz')
All inputs are finite; a program needn't handle non-finite values.
Results may differ from a plain program's by a relative error of at most 0.0013.
Values may be sent and summed in bfloat16 or wider, within the bound.
A program may use at most 192 MiB of HBM per device.

v0:
```python
import jax
import jax.numpy as jnp
from jax import lax
from jax.sharding import PartitionSpec as P


def passed_along(array, axis, by):
    size = lax.axis_size(axis)
    pairs = [(i, i + by) for i in range(size) if 0 <= i + by < size]
    return lax.ppermute(array, axis, pairs)


def extended(array, sides, width):
    for axis, dim in sides:
        size, length = (lax.axis_size(axis), array.shape[dim])
        up = [(i, (i + 1) % size) for i in range(size - 1)]
        down = [(j, i) for i, j in up]
        last = lax.slice_in_dim(array, length - width, length, axis=dim)
        first = lax.slice_in_dim(array, 0, width, axis=dim)
        before = lax.ppermute(last, axis, up)
        after = lax.ppermute(first, axis, down)
        array = jnp.concatenate([before, array, after], axis=dim)
    return array


def gaussian(offsets, length):
    centre = (length - 1) / 2.0
    spread = length / 8.0
    return jnp.exp(-((offsets - centre) ** 2) / (2.0 * spread * spread))


def place_halves(values, axis_k, axis_h):
    leading = lax.index_in_dim(values, 0, axis_h, keepdims=False)
    trailing = lax.index_in_dim(values, 1, axis_h, keepdims=False)
    lead_pad = [(0, 0)] * leading.ndim
    trail_pad = [(0, 0)] * leading.ndim
    lead_pad[axis_k] = (0, 1)
    trail_pad[axis_k] = (1, 0)
    return jnp.pad(leading, lead_pad) + jnp.pad(trailing, trail_pad)


def fold_volume(weighted, stride):
    count_a, count_b, classes, length, _, depth = weighted.shape
    count_c = depth // length
    folded = weighted.reshape(count_a, count_b, classes, length, length, count_c, 2, stride)
    folded = place_halves(folded, 5, 6)
    depth_cells = (count_c + 1) * stride
    folded = folded.reshape(count_a, count_b, classes, length, 2, stride, depth_cells)
    folded = place_halves(folded, 1, 4)
    wide_cells = (count_b + 1) * stride
    folded = folded.transpose(0, 2, 3, 1, 4, 5).reshape(
        count_a, classes, 2, stride, wide_cells, depth_cells
    )
    folded = place_halves(folded, 0, 2)
    return folded.transpose(1, 0, 2, 3, 4).reshape(
        classes, (count_a + 1) * stride, wide_cells, depth_cells
    )


def weight_line(begin_at, number, stride):
    cells = begin_at + jnp.arange(number, dtype=jnp.int32)
    cell_index = cells // stride
    near_offset = (cells - cell_index * stride).astype(jnp.float32)
    length = 2 * stride
    line = gaussian(near_offset, length)
    return line + jnp.where(cell_index >= 1, gaussian(near_offset + stride, length), 0.0)


def count_line(begin_at, number, extent):
    cells = begin_at + jnp.arange(number, dtype=jnp.int32)
    return 3.0 - (cells == 0).astype(jnp.float32) - (cells == extent - 1).astype(jnp.float32)


def per_device(patches):
    classes = patches.shape[2]
    length = patches.shape[4]
    stride = length // 2
    count_y = patches.shape[1]
    count_z = patches.shape[5] // length
    devices_x, devices_y, devices_z = (
        lax.axis_size("gx"),
        lax.axis_size("gy"),
        lax.axis_size("gz"),
    )
    index_x, index_y, index_z = (lax.axis_index("gx"), lax.axis_index("gy"), lax.axis_index("gz"))
    count_x = patches.shape[0] // devices_x
    profile = gaussian(jnp.arange(length).astype(jnp.float32), length)
    factor = (
        profile[:, None, None] * profile[None, :, None] * jnp.tile(profile, count_z)[None, None, :]
    )
    cells_x, cells_y, cells_z = (count_x * stride, count_y * stride, count_z * stride)
    regrouped = lax.all_to_all(patches, "gx", split_axis=0, concat_axis=3, tiled=True)
    weighted = regrouped.astype(jnp.float32) * factor
    volume = fold_volume(weighted, stride)
    arrived = passed_along(volume[:, cells_x:], "gx", 1)
    volume = jnp.concatenate([volume[:, :stride] + arrived, volume[:, stride:cells_x]], 1)
    arrived = passed_along(volume[:, :, cells_y:], "gy", 1)
    volume = jnp.concatenate([volume[:, :, :stride] + arrived, volume[:, :, stride:cells_y]], 2)
    upper_cells = jnp.moveaxis(volume[:, :, :, cells_z:], 3, 1).reshape(
        classes, stride, cells_x * cells_y
    )
    arrived = passed_along(upper_cells, "gz", 1)
    arrived = jnp.moveaxis(arrived.reshape(classes, stride, cells_x, cells_y), 1, 3)
    volume = jnp.concatenate(
        [volume[:, :, :, :stride] + arrived, volume[:, :, :, stride:cells_z]], 3
    )
    line_x = weight_line(index_x * cells_x, cells_x, stride)
    line_y = weight_line(index_y * cells_y, cells_y, stride)
    line_z = weight_line(index_z * cells_z, cells_z, stride)
    weight_sum = line_x[:, None, None] * line_y[None, :, None] * line_z[None, None, :]
    logits = volume / weight_sum
    probability = jax.nn.softmax(logits, axis=0)
    padded = extended(probability.astype(jnp.bfloat16), (("gz", 3),), 1).astype(probability.dtype)
    summed = padded[:, :, :, :-2] + padded[:, :, :, 1:-1] + padded[:, :, :, 2:]
    padded = extended(summed, (("gy", 2),), 1)
    summed = padded[:, :, :-2] + padded[:, :, 1:-1] + padded[:, :, 2:]
    padded = extended(summed, (("gx", 1),), 1)
    summed = padded[:, :-2] + padded[:, 1:-1] + padded[:, 2:]
    counts = count_line(index_x * cells_x, cells_x, cells_x * devices_x)[:, None, None]
    counts = counts * count_line(index_y * cells_y, cells_y, cells_y * devices_y)[None, :, None]
    counts = counts * count_line(index_z * cells_z, cells_z, cells_z * devices_z)[None, None, :]
    smooth = summed / counts
    return (smooth, jnp.max(smooth, axis=0))


def solution(mesh):
    in_specs = (P(None, "gy", None, "gx", None, "gz"),)
    out_specs = (P(None, "gx", "gy", "gz"), P("gx", "gy", "gz"))
    return jax.shard_map(
        per_device, mesh=mesh, in_specs=in_specs, out_specs=out_specs, check_vma=False
    )
```

profile of v0, /device:TPU:89, one launch (start us, length us, event | category | flops | bytes accessed | tf_op | source)
XLA Modules:
  0.0 316.0 jit_solution(11625888725608442333)
XLA Ops:
  0.6 8.5 %all-to-all-start = ((bf16[16,1,3,4,64,128]{5,4,3,2,1,0:T(8,128)(2,1)}), bf16[16,1,3,4,64,128]{5,4,3,2,1,0:T(8,128)(2,1)S(1)}, u32[]{:S(2)}, u32[]{:S(2)}) async-start(bf16[16,1,3,4,64,128]{5,4,3,2,1,0:T(8,128)(2,1)} %param.1), calls=%async_computation | async-start | bytes 6291456 | tf_op jit(solution)/shard_map/all_to_all | solution.py:92
  9.2 2.6 broadcast_multiply_fusion.1
  11.8 69.1 %all-to-all-done = bf16[16,1,3,4,64,128]{5,4,3,2,1,0:T(8,128)(2,1)S(1)} async-done(((bf16[16,1,3,4,64,128]{5,4,3,2,1,0:T(8,128)(2,1)}), bf16[16,1,3,4,64,128]{5,4,3,2,1,0:T(8,128)(2,1)S(1)}, u32[]{:S(2)}, u32[]{:S(2)}) %all-to-all-start) | async-done | bytes 3145760 | tf_op jit(solution)/shard_map/all_to_all | solution.py:92
  80.9 4.6 %copy.19 = bf16[16,1,3,4,64,128]{4,5,3,0,2,1:T(8,128)(2,1)} copy(bf16[16,1,3,4,64,128]{5,4,3,2,1,0:T(8,128)(2,1)S(1)} %all-to-all-done) | data formatting | bytes 6291456 | tf_op jit(solution)/shard_map/all_to_all | solution.py:92
  85.4 8.8 %bitcast_convert_fusion = f32[16,1,1,3,4,64,128]{5,6,4,0,3,2,1:T(8,128)} fusion(bf16[16,1,3,4,64,128]{4,5,3,0,2,1:T(8,128)(2,1)} %copy.19), kind=kLoop, calls=%fused_computation.4 | loop fusion | flops 1572864 | bytes 9437184 | tf_op jit(solution)/shard_map/convert_element_type | solution.py:93
  94.2 13.9 %broadcast_multiply_fusion = f32[1,1,3,64,64,2,2,32]{4,7,6,5,3,2,1,0:T(8,128)} fusion(f32[1,1,3,64,64,2,2,32]{4,7,6,5,3,2,1,0:T(8,128)} %bitcast.37, f32[64,64,2,2,32]{1,4,3,2,0:T(8,128)} %broadcast_multiply_fusion.1), kind=kLoop, calls=%fused_computation.6 | loop fusion | flops 1572864 | bytes 14680064 | tf_op jit(solution)/shard_map/mul | solution.py:93
  108.2 9.6 %slice_bitcast_fusion.1 = (f32[1,1,3,64,64,2,32]{4,6,5,3,2,1,0:T(8,128)S(1)}, f32[1,1,3,64,64,2,32]{4,6,5,3,2,1,0:T(8,128)}) fusion(f32[1,1,3,64,64,2,2,32]{4,7,6,5,3,2,1,0:T(8,128)} %broadcast_multiply_fusion), kind=kLoop, calls=%fused_computation.3 | loop fusion | bytes 12582912 | tf_op jit(solution)/shard_map/squeeze | solution.py:33
  117.7 8.2 %pad_add_fusion = f32[1,1,3,64,64,3,32]{4,6,5,3,2,1,0:T(8,128)} fusion(f32[1,1,3,64,64,2,32]{4,6,5,3,2,1,0:T(8,128)} %get-tuple-element.7, f32[1,1,3,64,64,2,32]{4,6,5,3,2,1,0:T(8,128)S(1)} %get-tuple-element.6), kind=kLoop, calls=%fused_computation.1 | loop fusion | flops 1179648 | bytes 11010048 | tf_op jit(solution)/shard_map/add | solution.py:39
  126.0 11.0 %copy.21 = f32[1,1,3,64,64,3,32]{3,6,5,4,2,1,0:T(8,128)} copy(f32[1,1,3,64,64,3,32]{4,6,5,3,2,1,0:T(8,128)} %pad_add_fusion) | data formatting | bytes 9437184 | tf_op jit(solution)/shard_map/add | solution.py:39
  137.0 4.6 %slice_bitcast_fusion.3 = (f32[1,1,3,64,32,96]{3,5,4,2,1,0:T(8,128)S(1)}, f32[1,1,3,64,32,96]{3,5,4,2,1,0:T(8,128)S(1)}) fusion(f32[1,1,3,64,2,32,96]{3,6,5,4,2,1,0:T(8,128)} %bitcast.38), kind=kLoop, calls=%fused_computation.8 | loop fusion | bytes 9437184 | tf_op jit(solution)/shard_map/squeeze | solution.py:33
  141.6 4.7 %add_bitcast_fusion = f32[1,3,64,2,32,96]{2,5,4,1,3,0:T(8,128)} fusion(f32[1,1,3,64,32,96]{3,5,4,2,1,0:T(8,128)S(1)} %get-tuple-element.9, f32[1,1,3,64,32,96]{3,5,4,2,1,0:T(8,128)S(1)} %get-tuple-element.8), kind=kLoop, calls=%fused_computation | loop fusion | flops 1179648 | bytes 9437184 | tf_op jit(solution)/shard_map/transpose | solution.py:51
  146.3 9.4 %copy.23 = f32[1,3,64,2,32,96]{5,4,3,2,1,0:T(8,128)} copy(f32[1,3,64,2,32,96]{2,5,4,1,3,0:T(8,128)} %add_bitcast_fusion) | data formatting | bytes 9437184 | tf_op jit(solution)/shard_map/transpose | solution.py:51
  155.8 3.4 %slice_bitcast_fusion.5 = (f32[1,3,32,64,96]{4,3,2,1,0:T(8,128)S(1)}, f32[1,3,32,64,96]{4,3,2,1,0:T(8,128)S(1)}) fusion(f32[1,3,2,32,64,96]{5,4,3,2,1,0:T(8,128)} %bitcast.41), kind=kLoop, calls=%fused_computation.11 | loop fusion | bytes 9437184 | tf_op jit(solution)/shard_map/squeeze | solution.py:33
  159.2 1.4 add_bitcast_fusion.1
  160.5 1.1 copy.25
  161.9 2.2 collective-permute-start
  164.1 68.6 %collective-permute-done = f32[3,32,64,96]{3,2,1,0:T(8,128)S(1)} collective-permute-done((f32[3,32,64,96]{3,2,1,0:T(8,128)S(1)}, f32[3,32,64,96]{3,2,1,0:T(8,128)S(1)}, u32[]{:S(2)}, u32[]{:S(2)}) %collective-permute-start) | collective-permute-done | bytes 2359328 | tf_op jit(solution)/shard_map/ppermute | solution.py:10
  232.7 0.7 slice_add_fusion
  233.5 1.5 copy-done
  235.0 4.3 %collective-permute-start.1 = (f32[3,32,32,96]{3,2,1,0:T(8,128)S(1)}, f32[3,32,32,96]{3,2,1,0:T(8,128)S(1)}, u32[]{:S(2)}, u32[]{:S(2)}) collective-permute-start(f32[3,32,32,96]{3,2,1,0:T(8,128)S(1)} %slice.117), channel_id=1, source_target_pairs={{0,2},{2,4},{4,6},{6,8},{8,10},{10,12},{12,14},{1,3},{3,5},{5,7},{... | collective-permute-start | bytes 3538952 | tf_op jit(solution)/shard_map/ppermute | solution.py:10
  239.4 33.3 %collective-permute-done.1 = f32[3,32,32,96]{3,2,1,0:T(8,128)S(1)} collective-permute-done((f32[3,32,32,96]{3,2,1,0:T(8,128)S(1)}, f32[3,32,32,96]{3,2,1,0:T(8,128)S(1)}, u32[]{:S(2)}, u32[]{:S(2)}) %collective-permute-start.1) | collective-permute-done | bytes 1179680 | tf_op jit(solution)/shard_map/ppermute | solution.py:10
  272.7 1.8 slice_add_fusion.4
  274.5 0.5 slice.119
  274.9 0.4 copy.26
  275.4 1.3 collective-permute-start.2
  276.8 1.0 broadcast_multiply_fusion.3
  277.8 3.6 %collective-permute-done.2 = f32[3,32,1024]{2,1,0:T(8,128)} collective-permute-done((f32[3,32,1024]{2,1,0:T(8,128)S(1)}, f32[3,32,1024]{2,1,0:T(8,128)}, u32[]{:S(2)}, u32[]{:S(2)}) %collective-permute-start.2) | collective-permute-done | bytes 393248 | tf_op jit(solution)/shard_map/ppermute | solution.py:10
  281.4 1.5 copy.27
  282.9 0.7 slice_add_fusion.3
  283.9 0.5 fusion.17
  284.7 0.3 divide_convert_fusion
  285.0 0.3 fusion.20
  285.3 0.6 copy.28
  286.0 1.3 collective-permute-start.3
  287.3 0.6 copy.29
  287.9 3.0 collective-permute-start.4
  291.0 0.7 copy.30
  291.8 0.7 copy.31
  292.5 0.7 maximum_convert_fusion
  293.1 0.9 slice_add_fusion.1
  294.1 3.5 %collective-permute-start.5 = (f32[3,32,1,64]{3,2,1,0:T(1,128)S(1)}, f32[3,32,1,64]{3,2,1,0:T(1,128)S(1)}, u32[]{:S(2)}, u32[]{:S(2)}) collective-permute-start(f32[3,32,1,64]{3,2,1,0:T(1,128)S(1)} %get-tuple-element.14), channel_id=1, source_target_pairs={{0,2},{2,4},{4,6},{6,8},{8,10},{10,12},{12,14},{1,3},{3,5},{5,7},{... | collective-permute-start | bytes 73736 | tf_op jit(solution)/shard_map/ppermute | solution.py:20
  297.6 4.2 %collective-permute-start.6 = (f32[3,32,1,64]{3,2,1,0:T(1,128)S(1)}, f32[3,32,1,64]{3,2,1,0:T(1,128)S(1)}, u32[]{:S(2)}, u32[]{:S(2)}) collective-permute-start(f32[3,32,1,64]{3,2,1,0:T(1,128)S(1)} %get-tuple-element.15), channel_id=1, source_target_pairs={{2,0},{4,2},{6,4},{8,6},{10,8},{12,10},{14,12},{3,1},{5,3},{7,5},{... | collective-permute-start | bytes 73736 | tf_op jit(solution)/shard_map/ppermute | solution.py:21
  301.8 2.1 collective-permute-done.6
  303.9 0.6 fusion.3
  304.5 2.1 collective-permute-start.7
  306.6 4.1 %collective-permute-start.8 = (f32[3,1,32,64]{3,2,1,0:T(8,128)S(1)}, f32[3,1,32,64]{3,2,1,0:T(8,128)S(1)}, u32[]{:S(2)}, u32[]{:S(2)}) collective-permute-start(f32[3,1,32,64]{3,2,1,0:T(8,128)S(1)} %get-tuple-element.13), channel_id=1, source_target_pairs={{16,0},{32,16},{48,32},{64,48},{80,64},{96,80},{112,96},{128,112},... | collective-permute-start | bytes 73736 | tf_op jit(solution)/shard_map/ppermute | solution.py:21
  310.9 2.7 collective-permute-done.8
  313.7 2.3 fusion.15
  (22 shorter events, 1.6 us)
Async XLA Ops:
  0.6 80.2 %all-to-all-start = ((bf16[16,1,3,4,64,128]{5,4,3,2,1,0:T(8,128)(2,1)}), bf16[16,1,3,4,64,128]{5,4,3,2,1,0:T(8,128)(2,1)S(1)}, u32[]{:S(2)}, u32[]{:S(2)}) async-start(bf16[16,1,3,4,64,128]{5,4,3,2,1,0:T(8,128)(2,1)} %param.1), calls=%async_computation | async-start | bytes 6291456 | tf_op jit(solution)/shard_map/all_to_all | solution.py:92
  161.9 70.8 %collective-permute-start = (f32[3,32,64,96]{3,2,1,0:T(8,128)S(1)}, f32[3,32,64,96]{3,2,1,0:T(8,128)S(1)}, u32[]{:S(2)}, u32[]{:S(2)}) collective-permute-start(f32[3,32,64,96]{3,2,1,0:T(8,128)S(1)} %slice.115), channel_id=1, source_target_pairs={{0,16},{16,32},{32,48},{48,64},{64,80},{80,96},{96,112},{112,128},... | collective-permute-start | bytes 7077896 | tf_op jit(solution)/shard_map/ppermute | solution.py:10
  233.3 1.6 copy-start
  235.0 37.7 %collective-permute-start.1 = (f32[3,32,32,96]{3,2,1,0:T(8,128)S(1)}, f32[3,32,32,96]{3,2,1,0:T(8,128)S(1)}, u32[]{:S(2)}, u32[]{:S(2)}) collective-permute-start(f32[3,32,32,96]{3,2,1,0:T(8,128)S(1)} %slice.117), channel_id=1, source_target_pairs={{0,2},{2,4},{4,6},{6,8},{8,10},{10,12},{12,14},{1,3},{3,5},{5,7},{... | collective-permute-start | bytes 3538952 | tf_op jit(solution)/shard_map/ppermute | solution.py:10
  275.4 6.0 %collective-permute-start.2 = (f32[3,32,1024]{2,1,0:T(8,128)S(1)}, f32[3,32,1024]{2,1,0:T(8,128)}, u32[]{:S(2)}, u32[]{:S(2)}) collective-permute-start(f32[3,32,1024]{2,1,0:T(8,128)S(1)} %copy.26), channel_id=1, source_target_pairs={{0,1},{2,3},{4,5},{6,7},{8,9},{10,11},{12,13},{14,15},{16,17},{18,... | collective-permute-start | bytes 1179656 | tf_op jit(solution)/shard_map/ppermute | solution.py:10
  282.8 1.0 copy-start.1
  286.0 5.0 %collective-permute-start.3 = (bf16[3,32,32,1]{2,1,3,0:T(8,128)(2,1)S(1)}, bf16[3,32,32,1]{2,1,3,0:T(8,128)(2,1)S(1)}, u32[]{:S(2)}, u32[]{:S(2)}) collective-permute-start(bf16[3,32,32,1]{2,1,3,0:T(8,128)(2,1)S(1)} %copy.28), channel_id=1, source_target_pairs={{0,1},{2,3},{4,5},{6,7},{8,9},{10,11},{12,13},{14,15},{16,17},{18,... | collective-permute-start | bytes 18440 | tf_op jit(solution)/shard_map/ppermute | solution.py:20
  287.9 3.9 %collective-permute-start.4 = (bf16[3,32,32,1]{2,1,3,0:T(8,128)(2,1)S(1)}, bf16[3,32,32,1]{2,1,3,0:T(8,128)(2,1)S(1)}, u32[]{:S(2)}, u32[]{:S(2)}) collective-permute-start(bf16[3,32,32,1]{2,1,3,0:T(8,128)(2,1)S(1)} %copy.29), channel_id=1, source_target_pairs={{1,0},{3,2},{5,4},{7,6},{9,8},{11,10},{13,12},{15,14},{17,16},{19,... | collective-permute-start | bytes 18440 | tf_op jit(solution)/shard_map/ppermute | solution.py:21
  294.1 7.7 %collective-permute-start.5 = (f32[3,32,1,64]{3,2,1,0:T(1,128)S(1)}, f32[3,32,1,64]{3,2,1,0:T(1,128)S(1)}, u32[]{:S(2)}, u32[]{:S(2)}) collective-permute-start(f32[3,32,1,64]{3,2,1,0:T(1,128)S(1)} %get-tuple-element.14), channel_id=1, source_target_pairs={{0,2},{2,4},{4,6},{6,8},{8,10},{10,12},{12,14},{1,3},{3,5},{5,7},{... | collective-permute-start | bytes 73736 | tf_op jit(solution)/shard_map/ppermute | solution.py:20
  297.6 6.3 %collective-permute-start.6 = (f32[3,32,1,64]{3,2,1,0:T(1,128)S(1)}, f32[3,32,1,64]{3,2,1,0:T(1,128)S(1)}, u32[]{:S(2)}, u32[]{:S(2)}) collective-permute-start(f32[3,32,1,64]{3,2,1,0:T(1,128)S(1)} %get-tuple-element.15), channel_id=1, source_target_pairs={{2,0},{4,2},{6,4},{8,6},{10,8},{12,10},{14,12},{3,1},{5,3},{7,5},{... | collective-permute-start | bytes 73736 | tf_op jit(solution)/shard_map/ppermute | solution.py:21
  304.5 6.4 %collective-permute-start.7 = (f32[3,1,32,64]{3,2,1,0:T(8,128)S(1)}, f32[3,1,32,64]{3,2,1,0:T(8,128)S(1)}, u32[]{:S(2)}, u32[]{:S(2)}) collective-permute-start(f32[3,1,32,64]{3,2,1,0:T(8,128)S(1)} %get-tuple-element.12), channel_id=1, source_target_pairs={{0,16},{16,32},{32,48},{48,64},{64,80},{80,96},{96,112},{112,128},... | collective-permute-start | bytes 73736 | tf_op jit(solution)/shard_map/ppermute | solution.py:20
  306.6 7.1 %collective-permute-start.8 = (f32[3,1,32,64]{3,2,1,0:T(8,128)S(1)}, f32[3,1,32,64]{3,2,1,0:T(8,128)S(1)}, u32[]{:S(2)}, u32[]{:S(2)}) collective-permute-start(f32[3,1,32,64]{3,2,1,0:T(8,128)S(1)} %get-tuple-element.13), channel_id=1, source_target_pairs={{16,0},{32,16},{48,32},{64,48},{80,64},{96,80},{112,96},{128,112},... | collective-permute-start | bytes 73736 | tf_op jit(solution)/shard_map/ppermute | solution.py:21
where the time goes:
time: 321 us; the launch traced here: 316 us
  waiting for transfers between devices  179 us (56%)
  local copies, waits for them, and re-layouts  51.3 us (16%)
  other arithmetic  49.8 us (16%)
  starting transfers between devices  34.5 us (11%)
    ppermute x3, waiting for transfers between devices, passed_along(): return lax.ppermute(array, axis, pairs)  105 us
    all_to_all x1, waiting for transfers between devices, per_device(): lax.all_to_all(patches, 'gx', split_axis=0, concat_axis=3, tiled=True)  69.1 us
    squeeze x3, local copies, waits for them, and re-layouts, place_halves(): leading = lax.index_in_dim(values, 0, axis_h, keepdims=False)  17.6 us
    mul x1, other arithmetic, per_device(): weighted = regrouped.astype(jnp.float32) * factor  13.9 us
    ppermute x3, starting transfers between devices, extended(): after = lax.ppermute(first, axis, down)  11.4 us
    add x1, local copies, waits for them, and re-layouts, place_halves(): return jnp.pad(leading, lead_pad) + jnp.pad(trailing, trail_pad)  11 us
    transpose x1, local copies, waits for them, and re-layouts, fold_volume(): folded.transpose(0, 2, 3, 1, 4, 5)  9.43 us
    convert_element_type x1, other arithmetic, per_device(): weighted = regrouped.astype(jnp.float32) * factor  8.79 us
  transfers between devices with their start and end apart: 10, of which 7 were waited for; matrix products, arithmetic and copies ran while one was open for 2% of the time, Pallas kernels for 0%

commit v1 on v0

v1 whole, which is shorter than its diff:
```python
import functools

import jax
import jax.numpy as jnp
from jax import lax
from jax.experimental import pallas as pl
from jax.experimental.pallas import tpu as pltpu
from jax.sharding import PartitionSpec as P

MESH = pl.DeviceIdType.MESH
F32 = jnp.float32
WIRE = jnp.float32


def gauss(offset):
    return jnp.exp(-((offset - 31.5) ** 2) / 128.0)


def filled(scalar, shape):
    return jnp.full(shape, scalar, F32)


def kernel(
    patches,
    smooth,
    conf,
    raw,
    part,
    weight,
    own,
    up_same,
    low_cross,
    up_cross,
    got_up_same,
    got_low_cross,
    got_up_cross,
    folded,
    slots,
    prob,
    column,
    got_column,
    rows,
    got_rows,
    summed,
    got_planes,
    load_sem,
    part_sem,
    x_send,
    x_recv,
    z_send,
    z_recv,
    h_send,
    h_recv,
):
    gx, gy, gz = lax.axis_index("gx"), lax.axis_index("gy"), lax.axis_index("gz")
    zc, xl = gx // 2, lax.rem(gx, 2)
    half = zc // 4
    xo = 1 - xl
    y_up, y_down = lax.rem(gy + 1, 8), lax.rem(gy + 7, 8)
    gx_up, gx_down = lax.rem(gx + 1, 16), lax.rem(gx + 15, 16)
    gx_cross = zc * 2 + xo
    partner = (gx, gy, 1 - gz)
    first = gz == 1

    def offset(k):
        odd = lax.rem(k, 2)
        return odd * ((9 + k) // 2) + (1 - odd) * ((8 - k) // 2)

    def target(k):
        return lax.rem(zc + offset(k), 8)

    def patch_of(k, side):
        a = 2 * target(k) + (xl if side == 0 else xo) - half
        return jnp.maximum(a, 0), (a >= 0).astype(F32)

    def load(k, side):
        a, _ = patch_of(k, side)
        return pltpu.make_async_copy(
            patches.at[a, 0], raw.at[2 * k + side], load_sem.at[2 * k + side]
        )

    def start_loads(k, _):
        load(k, 0).start()
        load(k, 1).start()
        return 0

    lax.fori_loop(0, 8, start_loads, 0)

    peers = [
        partner,
        (gx, y_up, gz),
        (gx, y_down, gz),
        (gx_cross, gy, gz),
        (gx_cross, y_up, gz),
        (gx_cross, y_down, gz),
        (lax.rem(gx + 15 + 2 * xl, 16), gy, gz),
    ]
    for d in range(1, 8):
        peers.append((lax.rem(gx + 2 * d, 16), gy, gz))
    barrier = pltpu.get_barrier_semaphore()
    for peer in peers:
        pl.semaphore_signal(barrier, inc=1, device_id=peer, device_id_type=MESH)

    lane = lax.broadcasted_iota(jnp.int32, (64, 128), 1)
    cell = lax.broadcasted_iota(jnp.int32, (64, 128), 0)
    plane = gauss(cell.astype(F32)) * gauss(lax.rem(lane, 64).astype(F32))
    sent_up = (gy < 7).astype(F32)
    plane = jnp.where(cell >= 32, plane * sent_up, plane)
    for u in range(4):
        row = (4 * gx + u).astype(F32)
        weight[u] = plane * gauss(filled(row, (64, 128)))

    pl.semaphore_wait(barrier, len(peers))

    def send_part(k, side):
        a, _ = patch_of(k, side)
        return pltpu.make_async_remote_copy(
            src_ref=patches.at[a, 0],
            dst_ref=part.at[2 * k + side],
            send_sem=part_sem.at[0, 2 * k + side],
            recv_sem=part_sem.at[1, 2 * k + side],
            device_id=partner,
            device_id_type=MESH,
        )

    @pl.when(gz == 0)
    def _():
        def start(k, _):
            send_part(k, 0).start()
            send_part(k, 1).start()
            return 0

        lax.fori_loop(0, 8, start, 0)

    quarter = lane // 32
    wrap_gain = jnp.where(
        (quarter == 0) | (quarter == 2), filled(first.astype(F32), (64, 128)), 1.0
    )
    last_quarter = lane >= 96
    from_part = last_quarter & (filled(first.astype(F32), (64, 128)) > 0.5)
    low_half = lane < 64
    outer = (quarter == 0) | (quarter == 3)

    def x_copies(k):
        t = target(k)
        plan = (
            (up_same, got_up_same, (gx, y_up, gz)),
            (low_cross, got_low_cross, (gx_cross, gy, gz)),
            (up_cross, got_up_cross, (gx_cross, y_up, gz)),
        )
        return [
            pltpu.make_async_remote_copy(
                src_ref=src.at[t],
                dst_ref=dst.at[t],
                send_sem=x_send.at[i, t],
                recv_sem=x_recv.at[i, t],
                device_id=device,
                device_id_type=MESH,
            )
            for i, (src, dst, device) in enumerate(plan)
        ]

    def fold(k, _):
        t = target(k)
        for side in (1, 0):
            load(k, side).wait()

            @pl.when(gz == 1)
            def _():
                send_part(k, side).wait_recv()

            _, valid = patch_of(k, side)
            for u in range(4):
                w = weight[u] * valid
                p = []
                for c in range(3):
                    mine = raw[2 * k + side, c, u].astype(F32)
                    theirs = part[2 * k + side, c, u].astype(F32)
                    p.append(jnp.where(from_part, theirs, mine))
                x1 = (p[1] - p[0]) * w
                x2 = (p[2] - p[0]) * w
                base = jnp.where(low_half, x1, pltpu.roll(x2, 64, 1))
                a1 = pltpu.roll(jnp.where(last_quarter, x1, x2), 32, 1)
                a2 = pltpu.roll(jnp.where(last_quarter, x2, x1), 96, 1)
                d = base + jnp.where(outer, a1, a2) * wrap_gain
                if side == 0:
                    own[t, u] = d[:32]
                    up_same[t, u] = d[32:]
                else:
                    low_cross[t, u] = d[:32]
                    up_cross[t, u] = d[32:]
        for copy in x_copies(k):
            copy.start()
        return 0

    lax.fori_loop(0, 8, fold, 0)

    def z_copy(k):
        t = target(k)
        return pltpu.make_async_remote_copy(
            src_ref=folded.at[t],
            dst_ref=slots.at[zc],
            send_sem=z_send.at[t],
            recv_sem=z_recv.at[zc],
            device_id=(2 * t + xl, gy, gz),
            device_id_type=MESH,
        )

    def forward(k, dst):
        t = target(k)
        for copy in x_copies(k):
            copy.wait_recv()
        place = t if dst is folded else zc
        dst[place, pl.ds(4 * xl, 4)] = own[t] + got_up_same[t]
        dst[place, pl.ds(4 * xo, 4)] = got_low_cross[t] + got_up_cross[t]

    def pass_on(k, _):
        forward(k, folded)
        z_copy(k).start()
        return 0

    lax.fori_loop(0, 7, pass_on, 0)
    forward(jnp.int32(7), slots)

    lane = lax.broadcasted_iota(jnp.int32, (32, 128), 1)
    cell = lax.broadcasted_iota(jnp.int32, (32, 128), 0)

    def line(offsets, later):
        return gauss(offsets) + later * gauss(offsets + 32.0)

    line_y = line(cell.astype(F32), (gy >= 1).astype(F32))
    z_later = jnp.where(lax.rem(lane, 64) >= 32, 1.0, filled(first.astype(F32), (32, 128)))
    line_z = line(lax.rem(lane, 32).astype(F32), z_later)
    x_later = (gx >= 1).astype(F32)

    def await_slot(s):
        @pl.when(zc != s)
        def _():
            pltpu.make_async_remote_copy(
                src_ref=folded.at[0],
                dst_ref=slots.at[s],
                send_sem=z_send.at[0],
                recv_sem=z_recv.at[s],
                device_id=(gx, gy, 1 - gz),
                device_id_type=MESH,
            ).wait_recv()

    def softmax(s, _):
        await_slot(s)
        await_slot(s + 4)
        for i in range(8):
            x = 8 * s + i
            total = slots[s, i] + slots[s + 4, i]
            line_x = line(filled(x.astype(F32), (32, 128)), x_later)
            d = total / (line_x * line_y * line_z)
            top = jnp.maximum(jnp.maximum(d, pltpu.roll(d, 64, 1)), 0.0)
            e = jnp.exp(d - top)
            prob[x] = e / (e + pltpu.roll(e, 64, 1) + jnp.exp(-top))
        return 0

    lax.fori_loop(0, 4, softmax, 0)

    is_first = filled(first.astype(F32), (32, 128))
    in_lane = lax.rem(lane, 64)
    shift_out = 65 * (1 - gz)
    shift_in = 63 + 65 * gz

    def pack(x, packed):
        moved = pltpu.roll(prob[x], x + shift_out, 1)
        return jnp.where(in_lane == x, moved, packed)

    column[...] = lax.fori_loop(0, 32, pack, jnp.zeros((32, 128), F32))

    def exchange(i, src, dst, device):
        return pltpu.make_async_remote_copy(
            src_ref=src,
            dst_ref=dst,
            send_sem=h_send.at[i],
            recv_sem=h_recv.at[i],
            device_id=device,
            device_id_type=MESH,
        )

    z_halo = exchange(0, column, got_column, partner)
    z_halo.start()
    z_halo.wait()

    def sum_z(x, _):
        p = prob[x]
        edge = pltpu.roll(got_column[...], lax.rem(shift_in - x, 128), 1)
        before = jnp.where(in_lane == 0, edge * is_first, pltpu.roll(p, 1, 1))
        after = jnp.where(in_lane == 63, edge * (1.0 - is_first), pltpu.roll(p, 127, 1))
        total = before + p + after
        prob[x] = total
        rows[0, pl.ds(x, 1)] = total[0:1]
        rows[1, pl.ds(x, 1)] = total[31:32]
        return 0

    lax.fori_loop(0, 32, sum_z, 0)
    y_halo = [
        exchange(1, rows.at[0], got_rows.at[1], (gx, y_down, gz)),
        exchange(2, rows.at[1], got_rows.at[0], (gx, y_up, gz)),
    ]
    for copy in y_halo:
        copy.start()
    for copy in y_halo:
        copy.wait()
    y_before, y_after = (gy > 0).astype(F32), (gy < 7).astype(F32)

    def sum_y(x, _):
        s = prob[x]
        low = jnp.broadcast_to(got_rows[0, pl.ds(x, 1)] * y_before, (32, 128))
        high = jnp.broadcast_to(got_rows[1, pl.ds(x, 1)] * y_after, (32, 128))
        before = jnp.where(cell == 0, low, pltpu.roll(s, 1, 0))
        after = jnp.where(cell == 31, high, pltpu.roll(s, 31, 0))
        summed[x + 1] = before + s + after
        return 0

    lax.fori_loop(0, 32, sum_y, 0)
    x_halo = [
        exchange(3, summed.at[1], got_planes.at[1], (gx_down, gy, gz)),
        exchange(4, summed.at[32], got_planes.at[0], (gx_up, gy, gz)),
    ]
    for copy in x_halo:
        copy.start()
    for copy in x_halo:
        copy.wait()
    summed[0] = got_planes[0] * (gx > 0).astype(F32)
    summed[33] = got_planes[1] * (gx < 15).astype(F32)

    count_y = (
        3.0
        - jnp.where(cell == 0, 1.0 - y_before, 0.0)
        - jnp.where(cell == 31, 1.0 - y_after, 0.0)
    )
    count_z = (
        3.0
        - jnp.where(in_lane == 0, 1.0 - is_first, 0.0)
        - jnp.where(in_lane == 63, is_first, 0.0)
    )
    inverse = 1.0 / (count_y * count_z)

    def sum_x(x, _):
        total = summed[x] + summed[x + 1] + summed[x + 2]
        cut = ((gx == 0) & (x == 0)) | ((gx == 15) & (x == 31))
        count_x = 3.0 - filled(cut.astype(F32), (32, 128))
        s1 = total * (inverse / count_x)
        s2 = pltpu.roll(s1, 64, 1)
        s0 = 1.0 - s1 - s2
        smooth[0, x] = s0[:, :64]
        smooth[1, x] = s1[:, :64]
        smooth[2, x] = s2[:, :64]
        conf[x] = jnp.maximum(jnp.maximum(s0, s1), s2)[:, :64]
        return 0

    lax.fori_loop(0, 32, sum_x, 0)

    @pl.when(gz == 0)
    def _():
        def finish(k, _):
            send_part(k, 0).wait_send()
            send_part(k, 1).wait_send()
            return 0

        lax.fori_loop(0, 8, finish, 0)

    def finish(k, _):
        for copy in x_copies(k):
            copy.wait_send()
        return 0

    lax.fori_loop(0, 8, finish, 0)

    def finish_z(k, _):
        z_copy(k).wait_send()
        return 0

    lax.fori_loop(0, 7, finish_z, 0)


def per_device(patches):
    vmem = pltpu.VMEM
    dma = pltpu.SemaphoreType.DMA
    any_space = pl.BlockSpec(memory_space=pl.ANY)
    in_vmem = pl.BlockSpec(memory_space=pltpu.VMEM)
    return pl.pallas_call(
        kernel,
        name="stitch",
        out_shape=(
            jax.ShapeDtypeStruct((3, 32, 32, 64), F32),
            jax.ShapeDtypeStruct((32, 32, 64), F32),
        ),
        in_specs=[any_space],
        out_specs=(in_vmem, in_vmem),
        scratch_shapes=[
            vmem((16, 3, 4, 64, 128), jnp.bfloat16),
            vmem((16, 3, 4, 64, 128), jnp.bfloat16),
            vmem((4, 64, 128), F32),
            vmem((8, 4, 32, 128), F32),
            *[vmem((8, 4, 32, 128), WIRE)] * 6,
            vmem((8, 8, 32, 128), WIRE),
            vmem((8, 8, 32, 128), WIRE),
            vmem((32, 32, 128), F32),
            vmem((32, 128), F32),
            vmem((32, 128), F32),
            vmem((2, 32, 128), F32),
            vmem((2, 32, 128), F32),
            vmem((34, 32, 128), F32),
            vmem((2, 32, 128), F32),
            dma((16,)),
            dma((2, 16)),
            dma((3, 8)),
            dma((3, 8)),
            dma((8,)),
            dma((8,)),
            dma((5,)),
            dma((5,)),
        ],
        compiler_params=pltpu.CompilerParams(
            collective_id=0, has_side_effects=True, vmem_limit_bytes=60 << 20
        ),
    )(patches)


def solution(mesh):
    in_specs = (P(None, "gy", None, "gx", None, "gz"),)
    out_specs = (P(None, "gx", "gy", "gz"), P("gx", "gy", "gz"))
    return jax.shard_map(
        per_device, mesh=mesh, in_specs=in_specs, out_specs=out_specs, check_vma=False
    )
```

time: 321 us -> 66 us (0.21)
  the two profiles are of different devices: /device:TPU:89 before, /device:TPU:8 now
where the time goes in v1:
time: 66 us; the launch traced here: 65.9 us
  Pallas kernels  61.7 us (93%)
  local copies, waits for them, and re-layouts  3.52 us (5%)
    pallas_call x1, Pallas kernels, per_device(): pl.pallas_call(kernel, name='stitch', out_shape=(jax.ShapeDtypeStruct((3,...  61.7 us
    unnamed x4, local copies, waits for them, and re-layouts  3.52 us

profile of v1, /device:TPU:8, one launch (start us, length us, event | category | flops | bytes accessed | tf_op | source)
XLA Modules:
  0.0 65.9 jit_solution(11947498023590676018)
XLA Ops:
  0.6 61.7 %stitch.1 = (f32[3,32,32,64]{3,2,1,0:T(8,128)}, f32[32,32,64]{2,1,0:T(8,128)}) custom-call(bf16[16,1,3,4,64,128]{5,4,3,2,1,0:T(8,128)(2,1)} %patches.1), custom_call_target="tpu_custom_call" | custom-call | tf_op jit(solution)/shard_map/stitch/pallas_call | solution.py:386
  62.4 0.0 copy-start
  62.4 2.7 %copy.5 = f32[3,32,32,64]{3,2,1,0:T(8,128)} copy(f32[3,32,32,64]{3,2,1,0:T(8,128)} %get-tuple-element.4) | data formatting | bytes 1572864
  65.1 0.0 copy-done
  65.1 0.8 %copy.6 = f32[32,32,64]{2,1,0:T(8,128)} copy(f32[32,32,64]{2,1,0:T(8,128)S(1)} %copy-done) | data formatting | bytes 524288
Async XLA Ops:
  62.4 2.7 %copy-start = (f32[32,32,64]{2,1,0:T(8,128)S(1)}, f32[32,32,64]{2,1,0:T(8,128)}, u32[]{:S(2)}) copy-start(f32[32,32,64]{2,1,0:T(8,128)} %get-tuple-element.5) | copy-start | bytes 786436

commit v2 on v1

v2 whole, which is shorter than its diff:
```python
import jax
import jax.numpy as jnp
from jax import lax
from jax.experimental import pallas as pl
from jax.experimental.pallas import tpu as pltpu
from jax.sharding import PartitionSpec as P

MESH = pl.DeviceIdType.MESH
F32 = jnp.float32
WIRE = jnp.bfloat16

BASE = 125.5
GAIN = 252.7 / 316.0
SPREAD = 0.05


def gauss(offset):
    return jnp.exp(-((offset - 31.5) ** 2) / 128.0)


def filled(scalar, shape):
    return jnp.full(shape, scalar, F32)


def encode(value, dither):
    size = jnp.exp2(jnp.abs(value) * GAIN + dither)
    return jnp.where(value < 0, -size, size).astype(WIRE)


def decode(code, dither):
    code = code.astype(F32)
    size = jnp.log2(jnp.abs(code)) * (1.0 / GAIN) - dither * (1.0 / GAIN)
    return jnp.where(code < 0, -size, size)


def share(offset):
    near = gauss(offset)
    return near / (near + gauss(offset + 32.0))


def kernel(
    patches,
    sums,
    side_sums,
    raw,
    part,
    own,
    up_same,
    low_cross,
    up_cross,
    got_up_same,
    got_low_cross,
    got_up_cross,
    folded,
    slots,
    dither,
    prob,
    got_block,
    rows,
    corners,
    got_planes,
    got_rows,
    got_corners,
    load_sem,
    part_sem,
    x_send,
    x_recv,
    z_send,
    z_recv,
    h_send,
    h_recv,
):
    gx, gy, gz = lax.axis_index("gx"), lax.axis_index("gy"), lax.axis_index("gz")
    zc, xl = gx // 2, lax.rem(gx, 2)
    half = zc // 4
    xo = 1 - xl
    gx_by = {1: lax.rem(gx + 1, 16), 0: gx, -1: lax.rem(gx + 15, 16)}
    gy_by = {1: lax.rem(gy + 1, 8), 0: gy, -1: lax.rem(gy + 7, 8)}
    gx_cross = zc * 2 + xo
    partner = (gx, gy, 1 - gz)

    def target(k):
        odd = lax.rem(k, 2)
        return lax.rem(zc + odd * ((9 + k) // 2) + (1 - odd) * ((8 - k) // 2), 8)

    def load(k, side):
        a = jnp.maximum(2 * target(k) + (xl if side == 0 else xo) - half, 0)
        return pltpu.make_async_copy(
            patches.at[a, 0], raw.at[2 * k + side], load_sem.at[2 * k + side]
        )

    def start_loads(k, _):
        load(k, 1).start()
        load(k, 0).start()
        return 0

    lax.fori_loop(0, 8, start_loads, 0)

    around = [(i, j) for i in (-1, 0, 1) for j in (-1, 0, 1) if i or j]
    peers = [partner]
    for i, j in around:
        peers.append((gx_by[i], gy_by[j], gz))
        peers.append((gx_by[i], gy_by[j], 1 - gz))
    for d in range(1, 8):
        peers.append((lax.rem(gx + 2 * d, 16), gy, gz))
    barrier = pltpu.get_barrier_semaphore()
    for peer in peers:
        pl.semaphore_signal(barrier, inc=1, device_id=peer, device_id_type=MESH)

    lane = lax.broadcasted_iota(jnp.int32, (64, 128), 1)
    core = filled(gz.astype(F32), (64, 128))
    offset = lax.rem(lane, 64).astype(F32)
    inner = lax.rem(lane, 32).astype(F32)
    weight = gauss(offset) / (gauss(inner) + gauss(inner + 32.0))
    weight = jnp.where(lane < 32, jnp.where(core > 0.5, weight, 1.0), weight)
    last_quarter = lane >= 96
    weight = jnp.where(last_quarter, weight * core, weight)
    from_part = last_quarter & (core > 0.5)
    low_half = lane < 64
    outer = (lane < 32) | last_quarter

    number = lax.broadcasted_iota(jnp.int32, (32, 128), 0) * 128 + lax.broadcasted_iota(
        jnp.int32, (32, 128), 1
    )
    for u in range(8):
        mixed = (number + 4096 * u + 1) * 40503
        mixed = (mixed + mixed // 512) * 30269
        bits = (mixed // 256) & 1023
        dither[u] = bits.astype(F32) * (SPREAD / 1024.0) - BASE

    def send_part(k, side):
        return pltpu.make_async_remote_copy(
            src_ref=raw.at[2 * k + side],
            dst_ref=part.at[2 * k + side],
            send_sem=part_sem.at[0, 2 * k + side],
            recv_sem=part_sem.at[1, 2 * k + side],
            device_id=partner,
            device_id_type=MESH,
        )

    def x_copies(k):
        t = target(k)
        plan = (
            (low_cross, got_low_cross, (gx_cross, gy, gz)),
            (up_cross, got_up_cross, (gx_cross, gy_by[1], gz)),
            (up_same, got_up_same, (gx, gy_by[1], gz)),
        )
        return [
            pltpu.make_async_remote_copy(
                src_ref=src.at[t],
                dst_ref=dst.at[t],
                send_sem=x_send.at[i, t],
                recv_sem=x_recv.at[i, t],
                device_id=device,
                device_id_type=MESH,
            )
            for i, (src, dst, device) in enumerate(plan)
        ]

    def fold(k, side):
        t = target(k)
        for u in range(4):
            p = []
            for c in range(3):
                mine = raw[2 * k + side, c, u].astype(F32)
                theirs = part[2 * k + side, c, u].astype(F32)
                p.append(jnp.where(from_part, theirs, mine))
            x1 = (p[1] - p[0]) * weight
            x2 = (p[2] - p[0]) * weight
            base = jnp.where(low_half, x1, pltpu.roll(x2, 64, 1))
            a1 = pltpu.roll(jnp.where(last_quarter, x1, x2), 32, 1)
            a2 = pltpu.roll(jnp.where(last_quarter, x2, x1), 96, 1)
            d = base + jnp.where(outer, a1, a2)
            if side == 0:
                own[t, u] = d[:32]
                up_same[t, u] = encode(d[32:], dither[u])
            else:
                low_cross[t, u] = encode(d[:32], dither[u])
                up_cross[t, u] = encode(d[32:], dither[u])

    def fold_early(k, _):
        for side in (1, 0):
            load(k, side).wait()
            fold(k, side)
        return 0

    lax.fori_loop(0, 8 * (1 - gz), fold_early, 0)
    pl.semaphore_wait(barrier, len(peers))

    @pl.when(gz == 0)
    def _():
        def start_part(k, _):
            send_part(k, 1).start()
            send_part(k, 0).start()
            return 0

        lax.fori_loop(0, 8, start_part, 0)

        def start_x(k, _):
            for copy in x_copies(k):
                copy.start()
            return 0

        lax.fori_loop(0, 8, start_x, 0)

    def fold_late(k, _):
        for side in (1, 0):
            load(k, side).wait()
            send_part(k, side).wait_recv()
            fold(k, side)
        for copy in x_copies(k):
            copy.start()
        return 0

    lax.fori_loop(0, 8 * gz, fold_late, 0)

    cell = lax.broadcasted_iota(jnp.int32, (32, 128), 0)
    has_below = filled((gy >= 1).astype(F32), (32, 128))
    high_y = (1.0 - share(cell.astype(F32))) * has_below
    low_y = 1.0 - high_y

    def z_copy(k):
        t = target(k)
        return pltpu.make_async_remote_copy(
            src_ref=folded.at[t],
            dst_ref=slots.at[zc],
            send_sem=z_send.at[t],
            recv_sem=z_recv.at[zc],
            device_id=(2 * t + xl, gy, gz),
            device_id_type=MESH,
        )

    def forward(k, dst, place):
        t = target(k)
        for copy in x_copies(k):
            copy.wait_recv()
        for u in range(4):
            same = low_y * own[t, u] + high_y * decode(got_up_same[t, u], dither[u])
            cross = low_y * decode(got_low_cross[t, u], dither[u])
            cross += high_y * decode(got_up_cross[t, u], dither[u])
            dst[place, 4 * xl + u] = encode(same, dither[4 + u])
            dst[place, 4 * xo + u] = encode(cross, dither[4 + u])

    def pass_on(k, _):
        forward(k, folded, target(k))
        z_copy(k).start()
        return 0

    lax.fori_loop(0, 7, pass_on, 0)
    forward(jnp.int32(7), slots, zc)

    def await_slot(s):
        @pl.when(zc != s)
        def _():
            pltpu.make_async_remote_copy(
                src_ref=folded.at[0],
                dst_ref=slots.at[s],
                send_sem=z_send.at[0],
                recv_sem=z_recv.at[s],
                device_id=partner,
                device_id_type=MESH,
            ).wait_recv()

    has_before = (gx >= 1).astype(F32)

    def softmax(s, _):
        await_slot(s)
        await_slot(s + 4)
        for i in range(8):
            x = 8 * s + i
            high_x = (1.0 - share(filled(x.astype(F32), (1, 128)))) * has_before
            near = decode(slots[s, i], dither[4 + i % 4])
            far = decode(slots[s + 4, i], dither[4 + i % 4])
            d = near + high_x * (far - near)
            top = jnp.maximum(jnp.maximum(d, pltpu.roll(d, 64, 1)), 0.0)
            e = jnp.exp(d - top)
            p = e / (e + pltpu.roll(e, 64, 1) + jnp.exp(-top))
            prob[x] = p
            rows[0, pl.ds(x, 1)] = p[0:1]
            rows[1, pl.ds(x, 1)] = p[31:32]
        return 0

    lax.fori_loop(0, 4, softmax, 0)
    for i in range(2):
        for j in range(2):
            corners[2 * i + j] = rows[j, 31 * i : 31 * i + 1]

    halos = []

    def exchange(src, dst, device):
        n = len(halos)
        halos.append(
            pltpu.make_async_remote_copy(
                src_ref=src,
                dst_ref=dst,
                send_sem=h_send.at[n],
                recv_sem=h_recv.at[n],
                device_id=device,
                device_id_type=MESH,
            )
        )
        halos[-1].start()

    for other in range(2):
        to = 1 - gz if other else gz
        for i in range(2):
            for j in range(2):
                exchange(
                    corners.at[2 * i + j],
                    got_corners.at[other, 2 * (1 - i) + 1 - j],
                    (gx_by[2 * i - 1], gy_by[2 * j - 1], to),
                )
    for other in range(2):
        to = 1 - gz if other else gz
        for i in range(2):
            exchange(rows.at[i], got_rows.at[other, 1 - i], (gx, gy_by[2 * i - 1], to))
        for i in range(2):
            exchange(
                prob.at[31 * i], got_planes.at[other, 1 - i], (gx_by[2 * i - 1], gy, to)
            )
    exchange(prob, got_block, partner)

    def sum_z(p, q):
        at = lax.rem(lax.broadcasted_iota(jnp.int32, p.shape, 1), 64)
        upper = filled(gz.astype(F32), p.shape)
        edge = pltpu.roll(q, 63 + 2 * gz, 1)
        before = jnp.where(at == 0, edge * upper, pltpu.roll(p, 1, 1))
        after = jnp.where(at == 63, edge * (1.0 - upper), pltpu.roll(p, 127, 1))
        return before + p + after

    halos[-1].wait_recv()

    def sum_block(s, _):
        for i in range(4):
            sums[4 * s + i + 1] = sum_z(prob[4 * s + i], got_block[4 * s + i])
        return 0

    lax.fori_loop(0, 8, sum_block, 0)
    for copy in halos[:-1]:
        copy.wait_recv()
    inside_x = ((gx > 0).astype(F32), (gx < 15).astype(F32))
    inside_y = ((gy > 0).astype(F32), (gy < 7).astype(F32))
    for i in range(2):
        sums[33 * i] = sum_z(got_planes[0, i], got_planes[1, i]) * inside_x[i]
    for j in range(2):
        side_sums[j, 1:33] = sum_z(got_rows[0, j], got_rows[1, j]) * inside_y[j]
        for i in range(2):
            n = 2 * i + j
            corner = sum_z(
                jnp.broadcast_to(got_corners[0, n], (8, 128)),
                jnp.broadcast_to(got_corners[1, n], (8, 128)),
            )
            side_sums[j, 33 * i : 33 * i + 1] = corner[0:1] * (inside_x[i] * inside_y[j])

    @pl.when(gz == 0)
    def _():
        def finish(k, _):
            send_part(k, 0).wait_send()
            send_part(k, 1).wait_send()
            return 0

        lax.fori_loop(0, 8, finish, 0)

    def finish(k, _):
        for copy in x_copies(k):
            copy.wait_send()
        return 0

    lax.fori_loop(0, 8, finish, 0)

    def finish_z(k, _):
        z_copy(k).wait_send()
        return 0

    lax.fori_loop(0, 7, finish_z, 0)
    for copy in halos:
        copy.wait_send()


def box(sums, side_sums, smooth, conf, sides):
    gx, gy, gz = lax.axis_index("gx"), lax.axis_index("gy"), lax.axis_index("gz")
    step = pl.program_id(0)
    count = smooth.shape[1]
    lane = lax.rem(lax.broadcasted_iota(jnp.int32, (32, 128), 1), 64)
    cell = lax.broadcasted_iota(jnp.int32, (32, 128), 0)

    def cut(place, at, there):
        return jnp.where(place == at, filled(there.astype(F32), (32, 128)), 0.0)

    count_y = 3.0 - cut(cell, 0, gy == 0) - cut(cell, 31, gy == 7)
    count_z = 3.0 - cut(lane, 0, gz == 0) - cut(lane, 63, gz == 1)
    inverse = 1.0 / (count_y * count_z)
    for j in range(2):
        sides[j] = side_sums[j, 0:32] + side_sums[j, 1:33] + side_sums[j, 2:34]
    for i in range(count):
        x = step * count + i
        s = sums[x] + sums[x + 1] + sums[x + 2]
        low = jnp.broadcast_to(sides[0, pl.ds(x, 1)], (32, 128))
        high = jnp.broadcast_to(sides[1, pl.ds(x, 1)], (32, 128))
        before = jnp.where(cell == 0, low, pltpu.roll(s, 1, 0))
        after = jnp.where(cell == 31, high, pltpu.roll(s, 31, 0))
        end = ((gx == 0) & (x == 0)) | ((gx == 15) & (x == 31))
        count_x = 3.0 - filled(end.astype(F32), (32, 128))
        s1 = (before + s + after) * (inverse / count_x)
        s2 = pltpu.roll(s1, 64, 1)
        s0 = 1.0 - s1 - s2
        smooth[0, i] = s0[:, :64]
        smooth[1, i] = s1[:, :64]
        smooth[2, i] = s2[:, :64]
        conf[i] = jnp.maximum(jnp.maximum(s0, s1), s2)[:, :64]


def per_device(patches):
    vmem = pltpu.VMEM
    dma = pltpu.SemaphoreType.DMA
    in_hbm = pl.BlockSpec(memory_space=pltpu.HBM)
    in_vmem = pl.BlockSpec(memory_space=pltpu.VMEM)
    sums, side_sums = pl.pallas_call(
        kernel,
        name="stitch",
        out_shape=(
            jax.ShapeDtypeStruct((34, 32, 128), F32),
            jax.ShapeDtypeStruct((2, 40, 128), F32),
        ),
        in_specs=[in_hbm],
        out_specs=(in_vmem, in_vmem),
        scratch_shapes=[
            vmem((16, 3, 4, 64, 128), jnp.bfloat16),
            vmem((16, 3, 4, 64, 128), jnp.bfloat16),
            vmem((8, 4, 32, 128), F32),
            *[vmem((8, 4, 32, 128), WIRE)] * 6,
            vmem((8, 8, 32, 128), WIRE),
            vmem((8, 8, 32, 128), WIRE),
            vmem((8, 32, 128), F32),
            vmem((32, 32, 128), F32),
            vmem((32, 32, 128), F32),
            vmem((2, 32, 128), F32),
            vmem((4, 1, 128), F32),
            vmem((2, 2, 32, 128), F32),
            vmem((2, 2, 32, 128), F32),
            vmem((2, 4, 1, 128), F32),
            dma((16,)),
            dma((2, 16)),
            dma((3, 8)),
            dma((3, 8)),
            dma((8,)),
            dma((8,)),
            dma((17,)),
            dma((17,)),
        ],
        compiler_params=pltpu.CompilerParams(
            collective_id=0, has_side_effects=True, vmem_limit_bytes=52 << 20
        ),
    )(patches)
    steps = 4
    return pl.pallas_call(
        box,
        name="box",
        grid=(steps,),
        out_shape=(
            jax.ShapeDtypeStruct((3, 32, 32, 64), F32),
            jax.ShapeDtypeStruct((32, 32, 64), F32),
        ),
        in_specs=[in_vmem, in_vmem],
        out_specs=(
            pl.BlockSpec((3, 32 // steps, 32, 64), lambda i: (0, i, 0, 0)),
            pl.BlockSpec((32 // steps, 32, 64), lambda i: (i, 0, 0)),
        ),
        scratch_shapes=[vmem((2, 32, 128), F32)],
        compiler_params=pltpu.CompilerParams(vmem_limit_bytes=20 << 20),
    )(sums, side_sums)


def solution(mesh):
    in_specs = (P(None, "gy", None, "gx", None, "gz"),)
    out_specs = (P(None, "gx", "gy", "gz"), P("gx", "gy", "gz"))
    return jax.shard_map(
        per_device, mesh=mesh, in_specs=in_specs, out_specs=out_specs, check_vma=False
    )
```

time: 66 us -> 41.3 us (0.63)
  the two profiles are of different devices: /device:TPU:8 before, /device:TPU:1 now
where the time goes in v2:
time: 41.3 us; the launch traced here: 41.2 us
  Pallas kernels  40.6 us (98%)
  between operations  0.64 us (2%)
    pallas_call x1, Pallas kernels, per_device(): pl.pallas_call(kernel, name='stitch', out_shape=(jax.ShapeDtypeStruct((34...  38.6 us
    pallas_call x1, Pallas kernels, per_device(): pl.pallas_call(box, name='box', grid=(steps,), out_shape=(jax.ShapeDtypeS...  2.04 us

profile of v2, /device:TPU:1, one launch (start us, length us, event | category | flops | bytes accessed | tf_op | source)
XLA Modules:
  0.0 41.2 jit_solution(4892850382073408862)
XLA Ops:
  0.6 38.6 %stitch.1 = (f32[34,32,128]{2,1,0:T(8,128)S(1)}, f32[2,40,128]{2,1,0:T(8,128)S(1)}) custom-call(bf16[16,1,3,4,64,128]{5,4,3,2,1,0:T(8,128)(2,1)} %patches.1), custom_call_target="tpu_custom_call" | custom-call | tf_op jit(solution)/shard_map/stitch/pallas_call | solution.py:418
  39.2 2.0 %box.1 = (f32[3,32,32,64]{3,2,1,0:T(8,128)}, f32[32,32,64]{2,1,0:T(8,128)}) custom-call(f32[34,32,128]{2,1,0:T(8,128)S(1)} %get-tuple-element.4.sums, f32[2,40,128]{2,1,0:T(8,128)S(1)} %get-tuple-element.5.side_sums), custom_call_target="tpu_custom_call" | custom-call | tf_op jit(solution)/shard_map/box/pallas_call | solution.py:456

commit v3 on v2

--- a/solution.py
+++ b/solution.py
@@ -12,6 +12,7 @@
 BASE = 125.5
 GAIN = 252.7 / 316.0
 SPREAD = 0.05
+LOG_SCALE = 1.0 / (GAIN * 0.6931471805599453)
 
 
 def gauss(offset):
@@ -29,7 +30,7 @@
 
 def decode(code, dither):
     code = code.astype(F32)
-    size = jnp.log2(jnp.abs(code)) * (1.0 / GAIN) - dither * (1.0 / GAIN)
+    size = jnp.log(jnp.abs(code)) * LOG_SCALE - dither * (1.0 / GAIN)
     return jnp.where(code < 0, -size, size)
 
 
@@ -43,7 +44,12 @@
     sums,
     side_sums,
     raw,
+    packed,
     part,
+    partial,
+    matrix,
+    part_matrix,
+    pick,
     own,
     up_same,
     low_cross,
@@ -61,6 +67,7 @@
     got_planes,
     got_rows,
     got_corners,
+    far_sem,
     load_sem,
     part_sem,
     x_send,
@@ -80,8 +87,11 @@
     partner = (gx, gy, 1 - gz)
 
     def target(k):
-        odd = lax.rem(k, 2)
-        return lax.rem(zc + odd * ((9 + k) // 2) + (1 - odd) * ((8 - k) // 2), 8)
+        near_order = jnp.where(k < 3, k + 4, jnp.where(k < 7, k - 3, 7))
+        k = jnp.where(half == 1, k, near_order)
+        other = (k < 4).astype(jnp.int32)
+        step = jnp.where(k == 4, 2, jnp.where(k == 5, 1, jnp.where(k == 6, 3, lax.rem(k, 7))))
+        return 4 * lax.rem(half + other, 2) + lax.rem(zc + step, 4)
 
     def load(k, side):
         a = jnp.maximum(2 * target(k) + (xl if side == 0 else xo) - half, 0)
@@ -96,41 +106,75 @@
 
     lax.fori_loop(0, 8, start_loads, 0)
 
+    there_x = {1: gx < 15, 0: gx >= 0, -1: gx > 0}
+    there_y = {1: gy < 7, 0: gy >= 0, -1: gy > 0}
     around = [(i, j) for i in (-1, 0, 1) for j in (-1, 0, 1) if i or j]
-    peers = [partner]
+    barrier = pltpu.get_barrier_semaphore()
+    pl.semaphore_signal(barrier, inc=1, device_id=partner, device_id_type=MESH)
     for i, j in around:
-        peers.append((gx_by[i], gy_by[j], gz))
-        peers.append((gx_by[i], gy_by[j], 1 - gz))
-    for d in range(1, 8):
-        peers.append((lax.rem(gx + 2 * d, 16), gy, gz))
-    barrier = pltpu.get_barrier_semaphore()
-    for peer in peers:
+
+        @pl.when(there_x[i] & there_y[j])
+        def _():
+            for to in (gz, 1 - gz):
+                peer = (gx_by[i], gy_by[j], to)
+                pl.semaphore_signal(barrier, inc=1, device_id=peer, device_id_type=MESH)
+
+    for d in range(1, 4):
+        peer = (2 * (4 * half + lax.rem(zc + d, 4)) + xl, gy, gz)
         pl.semaphore_signal(barrier, inc=1, device_id=peer, device_id_type=MESH)
 
-    lane = lax.broadcasted_iota(jnp.int32, (64, 128), 1)
-    core = filled(gz.astype(F32), (64, 128))
-    offset = lax.rem(lane, 64).astype(F32)
-    inner = lax.rem(lane, 32).astype(F32)
-    weight = gauss(offset) / (gauss(inner) + gauss(inner + 32.0))
-    weight = jnp.where(lane < 32, jnp.where(core > 0.5, weight, 1.0), weight)
-    last_quarter = lane >= 96
-    weight = jnp.where(last_quarter, weight * core, weight)
-    from_part = last_quarter & (core > 0.5)
-    low_half = lane < 64
-    outer = (lane < 32) | last_quarter
+    @pl.when(half == 0)
+    def _():
+        for d in range(4, 8):
+            peer = (2 * d + xl, gy, gz)
+            pl.semaphore_signal(barrier, inc=1, device_id=peer, device_id_type=MESH)
+
+    wide_x = 3 - (gx == 0).astype(jnp.int32) - (gx == 15).astype(jnp.int32)
+    wide_y = 3 - (gy == 0).astype(jnp.int32) - (gy == 7).astype(jnp.int32)
+    arrivals = 2 * (wide_x * wide_y - 1) + 1 + 3 + 4 * half
+
+    cell = lax.broadcasted_iota(jnp.int32, (128, 256), 0)
+    lane = lax.rem(lax.broadcasted_iota(jnp.int32, (128, 256), 1), 128)
+    leading = lax.broadcasted_iota(jnp.int32, (128, 256), 1) < 128
+    upper = filled(gz.astype(F32), (128, 256))
+
+    def two_terms(value):
+        head = value.astype(WIRE).astype(F32)
+        return jnp.where(leading, head, value - head).astype(WIRE)
+
+    inner = lax.rem(cell, 32).astype(F32)
+    weight = gauss(lax.rem(cell, 64).astype(F32)) / (gauss(inner) + gauss(inner + 32.0))
+    weight = jnp.where((cell < 32) & (upper < 0.5), 1.0, weight)
+    place = jnp.where(cell < 64, cell, cell - 32)
+    hit = (place == lax.rem(lane, 64)) & (cell < 96)
+    second = lane >= 64
+    weight = jnp.where(hit, weight, 0.0)
+    matrix[0:128] = two_terms(-weight)
+    matrix[128:256] = two_terms(jnp.where(second, 0.0, weight))
+    matrix[256:384] = two_terms(jnp.where(second, weight, 0.0))
+    weight = 1.0 - share(inner)
+    weight = jnp.where(lax.rem(cell, 32) == lax.rem(lane, 64), weight, 0.0)
+    chosen = jnp.where(second, 2, 1) == cell // 32
+    weight = jnp.where(cell < 32, -weight, jnp.where(chosen, weight, 0.0))
+    part_matrix[...] = two_terms(weight)
+    for c in range(3):
+        to = lax.broadcasted_iota(jnp.int32, (128, 128), 1) - 32 * c
+        at = lax.broadcasted_iota(jnp.int32, (128, 128), 0) - 96
+        pick[128 * c : 128 * c + 128] = jnp.where((at == to) & (at >= 0), 1.0, 0.0).astype(WIRE)
 
     number = lax.broadcasted_iota(jnp.int32, (32, 128), 0) * 128 + lax.broadcasted_iota(
         jnp.int32, (32, 128), 1
     )
     for u in range(8):
-        mixed = (number + 4096 * u + 1) * 40503
-        mixed = (mixed + mixed // 512) * 30269
-        bits = (mixed // 256) & 1023
+        mixed = (number + 4096 * u + 1) * -1640531535
+        mixed = (mixed ^ lax.shift_right_logical(mixed, 15)) * -2048144789
+        mixed = (mixed ^ lax.shift_right_logical(mixed, 13)) * -1028477387
+        bits = lax.shift_right_logical(mixed, 8) & 1023
         dither[u] = bits.astype(F32) * (SPREAD / 1024.0) - BASE
 
     def send_part(k, side):
         return pltpu.make_async_remote_copy(
-            src_ref=raw.at[2 * k + side],
+            src_ref=packed.at[2 * k + side],
             dst_ref=part.at[2 * k + side],
             send_sem=part_sem.at[0, 2 * k + side],
             recv_sem=part_sem.at[1, 2 * k + side],
@@ -157,67 +201,70 @@
             for i, (src, dst, device) in enumerate(plan)
         ]
 
-    def fold(k, side):
+    def cells(k, side):
+        classes = [raw[2 * k + side, c].reshape(256, 128) for c in range(3)]
+        return jnp.concatenate(classes, axis=1)
+
+    def product(left, right):
+        both = jnp.dot(left, right[...], preferred_element_type=F32)
+        return both[:, :128] + both[:, 128:]
+
+    def emit(k, side, d):
         t = target(k)
         for u in range(4):
-            p = []
-            for c in range(3):
-                mine = raw[2 * k + side, c, u].astype(F32)
-                theirs = part[2 * k + side, c, u].astype(F32)
-                p.append(jnp.where(from_part, theirs, mine))
-            x1 = (p[1] - p[0]) * weight
-            x2 = (p[2] - p[0]) * weight
-            base = jnp.where(low_half, x1, pltpu.roll(x2, 64, 1))
-            a1 = pltpu.roll(jnp.where(last_quarter, x1, x2), 32, 1)
-            a2 = pltpu.roll(jnp.where(last_quarter, x2, x1), 96, 1)
-            d = base + jnp.where(outer, a1, a2)
+            low, high = d[64 * u : 64 * u + 32], d[64 * u + 32 : 64 * u + 64]
             if side == 0:
-                own[t, u] = d[:32]
-                up_same[t, u] = encode(d[32:], dither[u])
+                own[t, u] = low
+                up_same[t, u] = encode(high, dither[u])
             else:
-                low_cross[t, u] = encode(d[:32], dither[u])
-                up_cross[t, u] = encode(d[32:], dither[u])
-
-    def fold_early(k, _):
+                low_cross[t, u] = encode(low, dither[u])
+                up_cross[t, u] = encode(high, dither[u])
+
+    pl.semaphore_wait(barrier, arrivals)
+
+    @pl.when(half == 1)
+    def _():
+        for d in range(4):
+            peer = (2 * d + xl, gy, gz)
+            pl.semaphore_signal(far_sem, inc=1, device_id=peer, device_id_type=MESH)
+
+    def start_x(k):
+        low, *high = x_copies(k)
+        low.start()
+
+        @pl.when(gy < 7)
+        def _():
+            for copy in high:
+                copy.start()
+
+    def fold_first(k, _):
         for side in (1, 0):
             load(k, side).wait()
-            fold(k, side)
-        return 0
-
-    lax.fori_loop(0, 8 * (1 - gz), fold_early, 0)
-    pl.semaphore_wait(barrier, len(peers))
-
-    @pl.when(gz == 0)
-    def _():
-        def start_part(k, _):
-            send_part(k, 1).start()
-            send_part(k, 0).start()
-            return 0
-
-        lax.fori_loop(0, 8, start_part, 0)
-
-        def start_x(k, _):
-            for copy in x_copies(k):
-                copy.start()
-            return 0
-
-        lax.fori_loop(0, 8, start_x, 0)
-
-    def fold_late(k, _):
+            picked = jnp.dot(cells(k, side), pick[...], preferred_element_type=F32)
+            packed[2 * k + side] = picked.astype(WIRE)
+            send_part(k, side).start()
+        for side in (1, 0):
+            emit(k, side, product(cells(k, side), matrix))
+        start_x(k)
+        return 0
+
+    def fold_second(k, _):
         for side in (1, 0):
             load(k, side).wait()
+            partial[side] = product(cells(k, side), matrix)
+        for side in (1, 0):
             send_part(k, side).wait_recv()
-            fold(k, side)
-        for copy in x_copies(k):
-            copy.start()
-        return 0
-
-    lax.fori_loop(0, 8 * gz, fold_late, 0)
+            more = product(part[2 * k + side], part_matrix)
+            emit(k, side, partial[side] + more)
+        start_x(k)
+        return 0
+
+    lax.fori_loop(0, 8 * (1 - gz), fold_first, 0)
+    lax.fori_loop(0, 8 * gz, fold_second, 0)
 
     cell = lax.broadcasted_iota(jnp.int32, (32, 128), 0)
-    has_below = filled((gy >= 1).astype(F32), (32, 128))
-    high_y = (1.0 - share(cell.astype(F32))) * has_below
-    low_y = 1.0 - high_y
+    has_below = filled((gy > 0).astype(F32), (32, 128)) > 0.5
+    high_y = 1.0 - share(cell.astype(F32))
 
     def z_copy(k):
         t = target(k)
@@ -232,12 +279,21 @@
 
     def forward(k, dst, place):
         t = target(k)
-        for copy in x_copies(k):
-            copy.wait_recv()
+        low, *high = x_copies(k)
+        low.wait_recv()
+
+        @pl.when(gy > 0)
+        def _():
+            for copy in high:
+                copy.wait_recv()
+
         for u in range(4):
-            same = low_y * own[t, u] + high_y * decode(got_up_same[t, u], dither[u])
-            cross = low_y * decode(got_low_cross[t, u], dither[u])
-            cross += high_y * decode(got_up_cross[t, u], dither[u])
+            same = own[t, u]
+            more = high_y * (decode(got_up_same[t, u], dither[u]) - same)
+            same += jnp.where(has_below, more, 0.0)
+            cross = decode(got_low_cross[t, u], dither[u])
+            more = high_y * (decode(got_up_cross[t, u], dither[u]) - cross)
+            cross += jnp.where(has_below, more, 0.0)
             dst[place, 4 * xl + u] = encode(same, dither[4 + u])
             dst[place, 4 * xo + u] = encode(cross, dither[4 + u])
 
@@ -246,7 +302,13 @@
         z_copy(k).start()
         return 0
 
-    lax.fori_loop(0, 7, pass_on, 0)
+    lax.fori_loop(0, 3, pass_on, 0)
+
+    @pl.when(half == 0)
+    def _():
+        pl.semaphore_wait(far_sem, 4)
+
+    lax.fori_loop(3, 7, pass_on, 0)
     forward(jnp.int32(7), slots, zc)
 
     def await_slot(s):
@@ -287,19 +349,19 @@
 
     halos = []
 
-    def exchange(src, dst, device):
+    def exchange(src, dst, i, j, to):
         n = len(halos)
-        halos.append(
-            pltpu.make_async_remote_copy(
-                src_ref=src,
-                dst_ref=dst,
-                send_sem=h_send.at[n],
-                recv_sem=h_recv.at[n],
-                device_id=device,
-                device_id_type=MESH,
-            )
+        copy = pltpu.make_async_remote_copy(
+            src_ref=src,
+            dst_ref=dst,
+            send_sem=h_send.at[n],
+            recv_sem=h_recv.at[n],
+            device_id=(gx_by[i], gy_by[j], to),
+            device_id_type=MESH,
         )
-        halos[-1].start()
+        out, back = there_x[i] & there_y[j], there_x[-i] & there_y[-j]
+        halos.append((copy, out, back))
+        pl.when(out)(copy.start)
 
     for other in range(2):
         to = 1 - gz if other else gz
@@ -308,17 +370,17 @@
                 exchange(
                     corners.at[2 * i + j],
                     got_corners.at[other, 2 * (1 - i) + 1 - j],
-                    (gx_by[2 * i - 1], gy_by[2 * j - 1], to),
+                    2 * i - 1,
+                    2 * j - 1,
+                    to,
                 )
     for other in range(2):
         to = 1 - gz if other else gz
         for i in range(2):
-            exchange(rows.at[i], got_rows.at[other, 1 - i], (gx, gy_by[2 * i - 1], to))
+            exchange(rows.at[i], got_rows.at[other, 1 - i], 0, 2 * i - 1, to)
         for i in range(2):
-            exchange(
-                prob.at[31 * i], got_planes.at[other, 1 - i], (gx_by[2 * i - 1], gy, to)
-            )
-    exchange(prob, got_block, partner)
+            exchange(prob.at[31 * i], got_planes.at[other, 1 - i], 2 * i - 1, 0, to)
+    exchange(prob, got_block, 0, 0, 1 - gz)
 
     def sum_z(p, q):
         at = lax.rem(lax.broadcasted_iota(jnp.int32, p.shape, 1), 64)
@@ -328,7 +390,7 @@
         after = jnp.where(at == 63, edge * (1.0 - upper), pltpu.roll(p, 127, 1))
         return before + p + after
 
-    halos[-1].wait_recv()
+    halos[-1][0].wait_recv()
 
     def sum_block(s, _):
         for i in range(4):
@@ -336,21 +398,26 @@
         return 0
 
     lax.fori_loop(0, 8, sum_block, 0)
-    for copy in halos[:-1]:
-        copy.wait_recv()
-    inside_x = ((gx > 0).astype(F32), (gx < 15).astype(F32))
-    inside_y = ((gy > 0).astype(F32), (gy < 7).astype(F32))
+    for copy, _, back in halos[:-1]:
+        pl.when(back)(copy.wait_recv)
+
+    def inside(value, condition):
+        return jnp.where(filled(condition.astype(F32), value.shape) > 0.5, value, 0.0)
+
     for i in range(2):
-        sums[33 * i] = sum_z(got_planes[0, i], got_planes[1, i]) * inside_x[i]
+        here = there_x[2 * i - 1]
+        sums[33 * i] = inside(sum_z(got_planes[0, i], got_planes[1, i]), here)
     for j in range(2):
-        side_sums[j, 1:33] = sum_z(got_rows[0, j], got_rows[1, j]) * inside_y[j]
+        here = there_y[2 * j - 1]
+        side_sums[j, 1:33] = inside(sum_z(got_rows[0, j], got_rows[1, j]), here)
         for i in range(2):
             n = 2 * i + j
             corner = sum_z(
                 jnp.broadcast_to(got_corners[0, n], (8, 128)),
                 jnp.broadcast_to(got_corners[1, n], (8, 128)),
             )
-            side_sums[j, 33 * i : 33 * i + 1] = corner[0:1] * (inside_x[i] * inside_y[j])
+            here = there_x[2 * i - 1] & there_y[2 * j - 1]
+            side_sums[j, 33 * i : 33 * i + 1] = inside(corner, here)[0:1]
 
     @pl.when(gz == 0)
     def _():
@@ -362,8 +429,14 @@
         lax.fori_loop(0, 8, finish, 0)
 
     def finish(k, _):
-        for copy in x_copies(k):
-            copy.wait_send()
+        low, *high = x_copies(k)
+        low.wait_send()
+
+        @pl.when(gy < 7)
+        def _():
+            for copy in high:
+                copy.wait_send()
+
         return 0
 
     lax.fori_loop(0, 8, finish, 0)
@@ -373,8 +446,8 @@
         return 0
 
     lax.fori_loop(0, 7, finish_z, 0)
-    for copy in halos:
-        copy.wait_send()
+    for copy, out, _ in halos:
+        pl.when(out)(copy.wait_send)
 
 
 def box(sums, side_sums, smooth, conf, sides):
@@ -426,7 +499,12 @@
         out_specs=(in_vmem, in_vmem),
         scratch_shapes=[
             vmem((16, 3, 4, 64, 128), jnp.bfloat16),
-            vmem((16, 3, 4, 64, 128), jnp.bfloat16),
+            vmem((16, 256, 128), WIRE),
+            vmem((16, 256, 128), WIRE),
+            vmem((2, 256, 128), F32),
+            vmem((384, 256), WIRE),
+            vmem((128, 256), WIRE),
+            vmem((384, 128), WIRE),
             vmem((8, 4, 32, 128), F32),
             *[vmem((8, 4, 32, 128), WIRE)] * 6,
             vmem((8, 8, 32, 128), WIRE),
@@ -439,6 +517,7 @@
             vmem((2, 2, 32, 128), F32),
             vmem((2, 2, 32, 128), F32),
             vmem((2, 4, 1, 128), F32),
+            pltpu.SemaphoreType.REGULAR,
             dma((16,)),
             dma((2, 16)),
             dma((3, 8)),

time: 41.3 us -> 38.1 us (0.923)
  the two profiles are of different devices: /device:TPU:1 before, /device:TPU:89 now
where the time goes in v3:
time: 38.1 us; the launch traced here: 38 us
  Pallas kernels  37.4 us (98%)
  between operations  0.64 us (2%)
    pallas_call x1, Pallas kernels, per_device(): pl.pallas_call(kernel, name='stitch', out_shape=(jax.ShapeDtypeStruct((34...  35.3 us
    pallas_call x1, Pallas kernels, per_device(): pl.pallas_call(box, name='box', grid=(steps,), out_shape=(jax.ShapeDtypeS...  2.04 us

profile of v3, /device:TPU:89, one launch (start us, length us, event | category | flops | bytes accessed | tf_op | source)
XLA Modules:
  0.0 38.0 jit_solution(3638643508497763201)
XLA Ops:
  0.6 35.3 %stitch.1 = (f32[34,32,128]{2,1,0:T(8,128)S(1)}, f32[2,40,128]{2,1,0:T(8,128)S(1)}) custom-call(bf16[16,1,3,4,64,128]{5,4,3,2,1,0:T(8,128)(2,1)} %patches.1), custom_call_target="tpu_custom_call" | custom-call | tf_op jit(solution)/shard_map/stitch/pallas_call | solution.py:491
  36.0 2.0 %box.1 = (f32[3,32,32,64]{3,2,1,0:T(8,128)}, f32[32,32,64]{2,1,0:T(8,128)}) custom-call(f32[34,32,128]{2,1,0:T(8,128)S(1)} %get-tuple-element.4.sums, f32[2,40,128]{2,1,0:T(8,128)S(1)} %get-tuple-element.5.side_sums), custom_call_target="tpu_custom_call" | custom-call | tf_op jit(solution)/shard_map/box/pallas_call | solution.py:535

commit v4 on v3

--- a/solution.py
+++ b/solution.py
@@ -8,6 +8,7 @@
 MESH = pl.DeviceIdType.MESH
 F32 = jnp.float32
 WIRE = jnp.bfloat16
+PARTS = 4
 
 BASE = 125.5
 GAIN = 252.7 / 316.0
@@ -104,7 +105,7 @@
         load(k, 0).start()
         return 0
 
-    lax.fori_loop(0, 8, start_loads, 0)
+    start_loads(jnp.int32(0), 0)
 
     there_x = {1: gx < 15, 0: gx >= 0, -1: gx > 0}
     there_y = {1: gy < 7, 0: gy >= 0, -1: gy > 0}
@@ -162,6 +163,7 @@
         at = lax.broadcasted_iota(jnp.int32, (128, 128), 0) - 96
         pick[128 * c : 128 * c + 128] = jnp.where((at == to) & (at >= 0), 1.0, 0.0).astype(WIRE)
 
+    lax.fori_loop(1, 8, start_loads, 0)
     number = lax.broadcasted_iota(jnp.int32, (32, 128), 0) * 128 + lax.broadcasted_iota(
         jnp.int32, (32, 128), 1
     )
@@ -259,9 +261,6 @@
         start_x(k)
         return 0
 
-    lax.fori_loop(0, 8 * (1 - gz), fold_first, 0)
-    lax.fori_loop(0, 8 * gz, fold_second, 0)
-
     cell = lax.broadcasted_iota(jnp.int32, (32, 128), 0)
     has_below = filled((gy > 0).astype(F32), (32, 128)) > 0.5
     high_y = 1.0 - share(cell.astype(F32))
@@ -298,17 +297,31 @@
             dst[place, 4 * xo + u] = encode(cross, dither[4 + u])
 
     def pass_on(k, _):
+        @pl.when((half == 0) & (k == 3))
+        def _():
+            pl.semaphore_wait(far_sem, 4)
+
         forward(k, folded, target(k))
         z_copy(k).start()
         return 0
 
-    lax.fori_loop(0, 3, pass_on, 0)
-
-    @pl.when(half == 0)
-    def _():
-        pl.semaphore_wait(far_sem, 4)
-
-    lax.fori_loop(3, 7, pass_on, 0)
+    def step(k, _):
+        @pl.when(gz == 0)
+        def _():
+            fold_first(k, 0)
+
+        @pl.when(gz == 1)
+        def _():
+            fold_second(k, 0)
+
+        @pl.when(k >= 3)
+        def _():
+            pass_on(k - 3, 0)
+
+        return 0
+
+    lax.fori_loop(0, 8, step, 0)
+    lax.fori_loop(5, 7, pass_on, 0)
     forward(jnp.int32(7), slots, zc)
 
     def await_slot(s):
@@ -450,10 +463,8 @@
         pl.when(out)(copy.wait_send)
 
 
-def box(sums, side_sums, smooth, conf, sides):
+def box(sums, side_sums, smooth, conf, sides, smooth_block, conf_block, sems):
     gx, gy, gz = lax.axis_index("gx"), lax.axis_index("gy"), lax.axis_index("gz")
-    step = pl.program_id(0)
-    count = smooth.shape[1]
     lane = lax.rem(lax.broadcasted_iota(jnp.int32, (32, 128), 1), 64)
     cell = lax.broadcasted_iota(jnp.int32, (32, 128), 0)
 
@@ -465,8 +476,8 @@
     inverse = 1.0 / (count_y * count_z)
     for j in range(2):
         sides[j] = side_sums[j, 0:32] + side_sums[j, 1:33] + side_sums[j, 2:34]
-    for i in range(count):
-        x = step * count + i
+
+    def plane(x):
         s = sums[x] + sums[x + 1] + sums[x + 2]
         low = jnp.broadcast_to(sides[0, pl.ds(x, 1)], (32, 128))
         high = jnp.broadcast_to(sides[1, pl.ds(x, 1)], (32, 128))
@@ -477,10 +488,31 @@
         s1 = (before + s + after) * (inverse / count_x)
         s2 = pltpu.roll(s1, 64, 1)
         s0 = 1.0 - s1 - s2
-        smooth[0, i] = s0[:, :64]
-        smooth[1, i] = s1[:, :64]
-        smooth[2, i] = s2[:, :64]
-        conf[i] = jnp.maximum(jnp.maximum(s0, s1), s2)[:, :64]
+        smooth_block[0, x] = s0[:, :64]
+        smooth_block[1, x] = s1[:, :64]
+        smooth_block[2, x] = s2[:, :64]
+        conf_block[x] = jnp.maximum(jnp.maximum(s0, s1), s2)[:, :64]
+
+    def copies(n):
+        part = pl.ds(n * (32 // PARTS), 32 // PARTS)
+        return (
+            pltpu.make_async_copy(smooth_block.at[:, part], smooth.at[:, part], sems.at[0, n]),
+            pltpu.make_async_copy(conf_block.at[part], conf.at[part], sems.at[1, n]),
+        )
+
+    for n in range(PARTS):
+
+        def some(x, _):
+            for i in range(4):
+                plane(4 * x + i)
+            return 0
+
+        lax.fori_loop(n * (8 // PARTS), (n + 1) * (8 // PARTS), some, 0)
+        for copy in copies(n):
+            copy.start()
+    for n in range(PARTS):
+        for copy in copies(n):
+            copy.wait()
 
 
 def per_device(patches):
@@ -531,21 +563,21 @@
             collective_id=0, has_side_effects=True, vmem_limit_bytes=52 << 20
         ),
     )(patches)
-    steps = 4
     return pl.pallas_call(
         box,
         name="box",
-        grid=(steps,),
         out_shape=(
             jax.ShapeDtypeStruct((3, 32, 32, 64), F32),
             jax.ShapeDtypeStruct((32, 32, 64), F32),
         ),
         in_specs=[in_vmem, in_vmem],
-        out_specs=(
-            pl.BlockSpec((3, 32 // steps, 32, 64), lambda i: (0, i, 0, 0)),
-            pl.BlockSpec((32 // steps, 32, 64), lambda i: (i, 0, 0)),
-        ),
-        scratch_shapes=[vmem((2, 32, 128), F32)],
+        out_specs=(in_hbm, in_hbm),
+        scratch_shapes=[
+            vmem((2, 32, 128), F32),
+            vmem((3, 32, 32, 64), F32),
+            vmem((32, 32, 64), F32),
+            dma((2, PARTS)),
+        ],
         compiler_params=pltpu.CompilerParams(vmem_limit_bytes=20 << 20),
     )(sums, side_sums)
 

time: 38.1 us -> 36.9 us (0.969)
  Pallas kernels: 37.4 us -> 36.2 us
    pallas_call x1, Pallas kernels: 35.3 us -> 34.5 us  [per_device(): pl.pallas_call(kernel, name='stitch', out_shape=(jax.ShapeDtypeStruct((34...]
where the time goes in v4:
time: 36.9 us; the launch traced here: 36.8 us
  Pallas kernels  36.2 us (98%)
  between operations  0.64 us (2%)
    pallas_call x1, Pallas kernels, per_device(): pl.pallas_call(kernel, name='stitch', out_shape=(jax.ShapeDtypeStruct((34...  34.5 us
    pallas_call x1, Pallas kernels, per_device(): pl.pallas_call(box, name='box', out_shape=(jax.ShapeDtypeStruct((3, 32, 3...  1.7 us

profile of v4, /device:TPU:89, one launch (start us, length us, event | category | flops | bytes accessed | tf_op | source)
XLA Modules:
  0.0 36.8 jit_solution(13135986016025415003)
XLA Ops:
  0.6 34.5 %stitch.1 = (f32[34,32,128]{2,1,0:T(8,128)S(1)}, f32[2,40,128]{2,1,0:T(8,128)S(1)}) custom-call(bf16[16,1,3,4,64,128]{5,4,3,2,1,0:T(8,128)(2,1)} %patches.1), custom_call_target="tpu_custom_call" | custom-call | tf_op jit(solution)/shard_map/stitch/pallas_call | solution.py:523
  35.1 1.7 %box.1 = (f32[3,32,32,64]{3,2,1,0:T(8,128)}, f32[32,32,64]{2,1,0:T(8,128)}) custom-call(f32[34,32,128]{2,1,0:T(8,128)S(1)} %get-tuple-element.4.sums, f32[2,40,128]{2,1,0:T(8,128)S(1)} %get-tuple-element.5.side_sums), custom_call_target="tpu_custom_call" | custom-call | tf_op jit(solution)/shard_map/box/pallas_call | solution.py:566

commit v5 on v4

--- a/solution.py
+++ b/solution.py
@@ -62,8 +62,10 @@
     slots,
     dither,
     prob,
+    block,
     got_block,
     rows,
+    sent_rows,
     corners,
     got_planes,
     got_rows,
@@ -351,11 +353,13 @@
             e = jnp.exp(d - top)
             p = e / (e + pltpu.roll(e, 64, 1) + jnp.exp(-top))
             prob[x] = p
+            block[x] = p.astype(WIRE)
             rows[0, pl.ds(x, 1)] = p[0:1]
             rows[1, pl.ds(x, 1)] = p[31:32]
         return 0
 
     lax.fori_loop(0, 4, softmax, 0)
+    sent_rows[...] = rows[0:2].astype(WIRE)
     for i in range(2):
         for j in range(2):
             corners[2 * i + j] = rows[j, 31 * i : 31 * i + 1]
@@ -390,12 +394,13 @@
     for other in range(2):
         to = 1 - gz if other else gz
         for i in range(2):
-            exchange(rows.at[i], got_rows.at[other, 1 - i], 0, 2 * i - 1, to)
+            exchange(sent_rows.at[i], got_rows.at[other, 1 - i], 0, 2 * i - 1, to)
         for i in range(2):
-            exchange(prob.at[31 * i], got_planes.at[other, 1 - i], 2 * i - 1, 0, to)
-    exchange(prob, got_block, 0, 0, 1 - gz)
+            exchange(block.at[31 * i], got_planes.at[other, 1 - i], 2 * i - 1, 0, to)
+    exchange(block, got_block, 0, 0, 1 - gz)
 
     def sum_z(p, q):
+        p, q = p.astype(F32), q.astype(F32)
         at = lax.rem(lax.broadcasted_iota(jnp.int32, p.shape, 1), 64)
         upper = filled(gz.astype(F32), p.shape)
         edge = pltpu.roll(q, 63 + 2 * gz, 1)
@@ -525,7 +530,7 @@
         name="stitch",
         out_shape=(
             jax.ShapeDtypeStruct((34, 32, 128), F32),
-            jax.ShapeDtypeStruct((2, 40, 128), F32),
+            jax.ShapeDtypeStruct((2, 48, 128), F32),
         ),
         in_specs=[in_hbm],
         out_specs=(in_vmem, in_vmem),
@@ -543,12 +548,14 @@
             vmem((8, 8, 32, 128), WIRE),
             vmem((8, 32, 128), F32),
             vmem((32, 32, 128), F32),
-            vmem((32, 32, 128), F32),
-            vmem((2, 32, 128), F32),
-            vmem((4, 1, 128), F32),
-            vmem((2, 2, 32, 128), F32),
-            vmem((2, 2, 32, 128), F32),
-            vmem((2, 4, 1, 128), F32),
+            vmem((32, 32, 128), WIRE),
+            vmem((32, 32, 128), WIRE),
+            vmem((3, 32, 128), F32),
+            vmem((2, 32, 128), WIRE),
+            vmem((16, 1, 128), F32),
+            vmem((2, 2, 32, 128), WIRE),
+            vmem((2, 2, 32, 128), WIRE),
+            vmem((4, 4, 1, 128), F32),
             pltpu.SemaphoreType.REGULAR,
             dma((16,)),
             dma((2, 16)),
@@ -573,7 +580,7 @@
         in_specs=[in_vmem, in_vmem],
         out_specs=(in_hbm, in_hbm),
         scratch_shapes=[
-            vmem((2, 32, 128), F32),
+            vmem((3, 32, 128), F32),
             vmem((3, 32, 32, 64), F32),
             vmem((32, 32, 64), F32),
             dma((2, PARTS)),

time: 36.9 us -> 36.2 us (0.981); the launches traced: 36.8 us -> 35.5 us
  Pallas kernels: 36.2 us -> 34.8 us
    pallas_call x1, Pallas kernels: 34.5 us -> 33.1 us  [per_device(): pl.pallas_call(kernel, name='stitch', out_shape=(jax.ShapeDtypeStruct((34...]
where the time goes in v5:
time: 36.2 us; the launch traced here: 35.5 us
  Pallas kernels  34.8 us (96%)
  between operations  0.64 us (2%)
    pallas_call x1, Pallas kernels, per_device(): pl.pallas_call(kernel, name='stitch', out_shape=(jax.ShapeDtypeStruct((34...  33.1 us
    pallas_call x1, Pallas kernels, per_device(): pl.pallas_call(box, name='box', out_shape=(jax.ShapeDtypeStruct((3, 32, 3...  1.7 us

profile of v5, /device:TPU:89, one launch (start us, length us, event | category | flops | bytes accessed | tf_op | source)
XLA Modules:
  0.0 35.5 jit_solution(8136615165121174308)
XLA Ops:
  0.6 33.1 %stitch.1 = (f32[34,32,128]{2,1,0:T(8,128)S(1)}, f32[2,48,128]{2,1,0:T(8,128)S(1)}) custom-call(bf16[16,1,3,4,64,128]{5,4,3,2,1,0:T(8,128)(2,1)} %patches.1), custom_call_target="tpu_custom_call" | custom-call | tf_op jit(solution)/shard_map/stitch/pallas_call | solution.py:528
  33.8 1.7 %box.1 = (f32[3,32,32,64]{3,2,1,0:T(8,128)}, f32[32,32,64]{2,1,0:T(8,128)}) custom-call(f32[34,32,128]{2,1,0:T(8,128)S(1)} %get-tuple-element.4.sums, f32[2,48,128]{2,1,0:T(8,128)S(1)} %get-tuple-element.5.side_sums), custom_call_target="tpu_custom_call" | custom-call | tf_op jit(solution)/shard_map/box/pallas_call | solution.py:573
